TPU v7x, 32 devices: a whole 2x2x4 slice. The times are simulated.
32 devices in a mesh: span: 2 (over y), height: 4 (over x, core), depth: 4 (over z).
Axes of the slice: x: 2, y: 2, z: 4, core: 2. Of those that a mesh axis runs over, the one named last changes fastest.
Arguments:
- load: float32 [8, 32, 64, 512], P(None, 'span', 'height', 'depth'), may hold values from -6 to 6
- phase: float32 [32, 64, 512], P('span', 'height', 'depth'), may hold values from 0.1 to 1
- void: int32 [4, 8, 64], P('span', 'height', 'depth'), may hold values from 0 to 1, as said below
- owner: int32 [4, 8, 64], P('span', 'height', 'depth'), may hold values from 0 to 1, as said below
- precond: bfloat16 [512, 512, 512], P(('span', 'height', 'depth')), may hold values from -1 to 2, as said below
Outputs:
- displacement: float32 [8, 32, 64, 512], P(None, 'span', 'height', 'depth')
- sensitivity: float32 [32, 64, 512], P('span', 'height', 'depth')
- phase_next: float32 [32, 64, 512], P('span', 'height', 'depth')
Inputs may be any that keep to these rules, and one draw needn't show every extreme that they name: `void`: each device's block of 16 x 16 x 128 cells holds at most 16 solid bricks; some device holds exactly 16. `owner`: among the solid bricks of one device at most 8 name any one value; on some device every value is named by exactly 8 solid bricks. Values of void bricks carry no meaning. `precond`: every block is symmetric with a positive diagonal that dominates each row.
All inputs are finite; a program needn't handle non-finite values.
Results may differ from a plain program's by a relative error of at most 0.0021.
Values may be sent and summed in bfloat16 or wider, within the bound.
No kernel may reach another device: no remote copies, remote signals or barrier semaphores. Data moves between devices by JAX's collectives and lax.ppermute only.
A program may use at most 128 MiB of HBM per device.

v0:
```python
import jax
import jax.numpy as jnp
from jax import lax
from jax.sharding import PartitionSpec as P

BE = 8
ITERS = 2
SWEEPS = 2
void_stiffness = 0.001
spring_rate = 0.05
time_step = 0.5
interface_weight = 0.5
epsilon_peak = 1e-06


def padded_2(block, sides, width):
    for axis, dim in sides:
        count = lax.axis_size(axis)
        forward = [(i, i + 1) for i in range(count - 1)]
        backward = [(target, source) for source, target in forward]
        low = lax.ppermute(
            lax.slice_in_dim(block, block.shape[dim] - width, None, axis=dim), axis, forward
        )
        high = lax.ppermute(lax.slice_in_dim(block, 0, width, axis=dim), axis, backward)
        block = jnp.concatenate([low, block, high], axis=dim)
    return block


def neighbours(padded):
    return [
        padded[..., 2:, 1:-1, 1:-1],
        padded[..., :-2, 1:-1, 1:-1],
        padded[..., 1:-1, 2:, 1:-1],
        padded[..., 1:-1, :-2, 1:-1],
        padded[..., 1:-1, 1:-1, 2:],
        padded[..., 1:-1, 1:-1, :-2],
    ]


def halo_stack(stacked):
    return padded_2(stacked, (("span", 1), ("height", 2), ("depth", 3)), 1)


def cell_sums(first, second):
    return jnp.sum(first * second, axis=(1, 2, 3))


def paired_sums(residual, search, image):
    return lax.psum(
        (cell_sums(residual, search), cell_sums(image, search)), ("span", "height", "depth")
    )


def local(load, phase, void, owner, precond):
    extents = phase.shape
    bricks_x, bricks_y, bricks_z = void.shape
    solid_bricks = (1 - void).astype(jnp.float32)
    expanded = jnp.broadcast_to(
        solid_bricks[:, None, :, None, :, None], (bricks_x, BE, bricks_y, BE, bricks_z, BE)
    )
    cell_mask = expanded.reshape(extents)
    stiffness = void_stiffness + (1.0 - void_stiffness) * phase**3
    coefficients = halo_stack(jnp.stack([cell_mask, cell_mask * stiffness]))
    near_pairs = neighbours(coefficients)
    weights = [cell_mask * 0.5 * (pair[0] * stiffness + pair[1]) for pair in near_pairs]

    def operate(field):
        padded = halo_stack(field)
        total = cell_mask * spring_rate * field
        for weight, near in zip(weights, neighbours(padded)):
            total = total + weight * (field - near)
        return (total, padded)

    span_count = lax.axis_size("span")
    slot_count = precond.shape[0]
    capacity = slot_count // span_count
    solid_flat = (1 - void).reshape(-1)
    owner_flat = owner.reshape(-1)
    columns = jnp.arange(span_count, dtype=jnp.int32)
    onehot = (owner_flat[:, None] == columns[None, :]).astype(jnp.int32) * solid_flat[:, None]
    before = jnp.cumsum(onehot, axis=0) - onehot
    rank = jnp.sum(before * onehot, axis=1)
    slot_of_brick = owner_flat * capacity + rank
    slot_ids = jnp.arange(slot_count, dtype=jnp.int32)
    matched = (slot_of_brick[None, :] == slot_ids[:, None]).astype(jnp.float32) * solid_flat[
        None, :
    ].astype(jnp.float32)
    selector = matched.reshape(slot_count, bricks_x, bricks_y, bricks_z)
    selector_low = selector.astype(jnp.bfloat16)
    loads = load.shape[0]

    def apply_blocks(incoming):
        image = jnp.einsum("sij,slj->sli", precond, incoming, preferred_element_type=jnp.float32)
        return lax.all_to_all(image, "span", split_axis=0, concat_axis=0, tiled=True)

    def precondition(residual):
        split = residual.astype(jnp.bfloat16).reshape(
            loads, bricks_x, BE, bricks_y, BE, bricks_z, BE
        )
        outgoing = jnp.einsum(
            "sxyz,lxiyjzk->slijk", selector_low, split, preferred_element_type=jnp.float32
        )
        outgoing = outgoing.astype(jnp.bfloat16).reshape(slot_count, loads, BE**3)
        returned = apply_blocks(
            lax.all_to_all(outgoing, "span", split_axis=0, concat_axis=0, tiled=True)
        )
        shaped = returned.reshape(slot_count, loads, BE, BE, BE)
        placed = jnp.einsum(
            "sxyz,slijk->lxiyjzk", selector, shaped, precision=lax.Precision.HIGHEST
        )
        return placed.reshape(loads, extents[0], extents[1], extents[2])

    right_side = cell_mask[None] * load
    solution = jnp.zeros_like(right_side)
    padded_solution = 0.0
    residual = right_side
    search = precondition(residual)
    image, padded_search = operate(search)
    norm_now, curvature_sum = paired_sums(residual, search, image)
    step_size = norm_now / curvature_sum
    direction = search
    padded_direction = padded_search
    along = image
    for iteration in range(ITERS):
        solution = solution + step_size[:, None, None, None] * direction
        padded_solution = padded_solution + step_size[:, None, None, None] * padded_direction
        residual = residual - step_size[:, None, None, None] * along
        if iteration + 1 < ITERS:
            search = precondition(residual)
            image, padded_search = operate(search)
            norm_next, curvature_sum = paired_sums(residual, search, image)
            factor = norm_next / norm_now
            step_size = norm_next / (curvature_sum - factor * norm_next / step_size)
            direction = search + factor[:, None, None, None] * direction
            padded_direction = padded_search + factor[:, None, None, None] * padded_direction
            along = image + factor[:, None, None, None] * along
            norm_now = norm_next
    solution_padded = halo_stack(solution)
    energy = jnp.zeros_like(phase)
    for pair, near in zip(near_pairs, neighbours(solution_padded)):
        energy = energy + pair[0] * jnp.sum((solution - near) ** 2, axis=0)
    sensitivity = -1.5 * (1.0 - void_stiffness) * phase**2 * cell_mask * energy
    peak_value = lax.pmax(jnp.max(-sensitivity), ("span", "height", "depth"))
    drive = (
        phase / time_step
        - 0.5 * phase * (1.0 - phase) * (1.0 - 2.0 * phase)
        - sensitivity / (peak_value + epsilon_peak)
    )
    inverse = 1.0 / (1.0 / time_step + 6.0 * interface_weight)
    current = phase
    for sweep_index in range(SWEEPS):
        padded = padded_2(
            current.astype(jnp.bfloat16), (("span", 0), ("height", 1), ("depth", 2)), 1
        ).astype(current.dtype)
        beside_all = neighbours(padded)
        current = (
            drive
            + interface_weight
            * (
                beside_all[0]
                + beside_all[1]
                + beside_all[2]
                + beside_all[3]
                + beside_all[4]
                + beside_all[5]
            )
        ) * inverse
    return (solution, sensitivity, current)


def solution(mesh):
    return jax.shard_map(
        local,
        mesh=mesh,
        in_specs=(
            P(None, "span", "height", "depth"),
            P("span", "height", "depth"),
            P("span", "height", "depth"),
            P("span", "height", "depth"),
            P(("span", "height", "depth"), None, None),
        ),
        out_specs=(
            P(None, "span", "height", "depth"),
            P("span", "height", "depth"),
            P("span", "height", "depth"),
        ),
        check_vma=False,
    )
```

profile of v0, /device:TPU:14, one launch (start us, length us, event | category | flops | bytes accessed | tf_op | source)
XLA Modules:
  0.0 461.7 jit_solution(4808410751461738423)
XLA Ops:
  10.2 10.6 %reshape.116 = bf16[8,2,8,2,8,16,8]{6,5,4,3,2,1,0:T(8,128)(2,1)} reshape(bf16[8,16,16,128]{3,2,1,0:T(8,128)(2,1)S(1)} %multiply_convert_fusion) | data formatting | bytes 1048576 | tf_op jit(solution)/shard_map/reshape | solution.py:97
  25.2 6.2 %bitcast_convert_fusion.1 = bf16[16,8,8,8,8]{0,4,3,2,1:T(8,128)(2,1)S(1)} fusion(bf16[8,2,8,2,8,16,8]{6,5,4,3,2,1,0:T(8,128)(2,1)} %reshape.116, f32[2,2,16]{2,1,0:T(2,128)S(1)} %copy-done.42, s32[2,2,16]{2,1,0:T(2,128)S(1)} %multiply_add_fusion.1), kind=kOutput, calls=%fused_computation.3 | convolution fusion | flops 8456192 | bytes 655872 | tf_op jit(solution)/shard_map/sxyz,lxiyjzk->slijk/dot_general | solution.py:100
  32.5 6.0 %all-to-all-start = ((bf16[16,8,512]{2,1,0:T(8,128)(2,1)}), bf16[16,8,512]{2,1,0:T(8,128)(2,1)S(1)}, u32[]{:S(2)}, u32[]{:S(2)}) async-start(bf16[16,8,512]{2,1,0:T(8,128)(2,1)} %copy.23), calls=%async_computation | async-start | bytes 262144 | tf_op jit(solution)/shard_map/all_to_all | solution.py:105
  39.6 3.5 collective-permute-start.10
  43.1 3.2 collective-permute-start.8
  46.3 6.4 %fusion.123 = f32[16,8,512]{2,1,0:T(8,128)} fusion(bf16[16,8,512]{2,1,0:T(8,128)(2,1)S(1)} %all-to-all-done, bf16[16,512,512]{2,1,0:T(8,128)(2,1)} %param.9), kind=kOutput, calls=%fused_computation.250 | convolution fusion | flops 67108864 | bytes 8781824 | tf_op jit(solution)/shard_map/sij,slj->sli/dot_general | solution.py:93
  52.7 4.6 all-to-all-start.1
  62.1 9.5 %convolution_bitcast_fusion.1 = f32[8,2,8,2,8,16,8]{5,6,3,1,4,2,0:T(8,128)} fusion(f32[16,8,8,8,8,1,1]{0,4,6,5,3,2,1:T(8,128)S(1)} %bitcast.148, f32[2,2,16]{2,1,0:T(2,128)} %copy-done.41, s32[2,2,16]{2,1,0:T(2,128)} %copy-done.44), kind=kOutput, calls=%fused_computation.1 | convolution fusion | flops 50333696 | bytes 1311232 | tf_op jit(solution)/shard_map/sxyz,slijk->lxiyjzk/dot_general | solution.py:108
  71.7 12.3 %copy.25 = f32[8,2,8,2,8,16,8]{6,5,4,3,2,1,0:T(8,128)} copy(f32[8,2,8,2,8,16,8]{5,6,3,1,4,2,0:T(8,128)} %convolution_bitcast_fusion.1) | data formatting | bytes 2097152 | tf_op jit(solution)/shard_map/sxyz,slijk->lxiyjzk/transpose | solution.py:108
  84.0 11.8 %reshape.119 = f32[8,16,16,128]{3,2,1,0:T(8,128)S(1)} reshape(f32[8,2,8,2,8,16,8]{6,5,4,3,2,1,0:T(8,128)} %copy.25) | data formatting | bytes 2097152 | tf_op jit(solution)/shard_map/reshape | solution.py:111
  98.0 4.5 collective-permute-start.1
  115.5 2.4 copy.28
  117.9 2.7 collective-permute-start.11
  123.1 3.1 collective-permute-start.9
  132.5 5.9 %multiply_reduce_fusion.1 = (f32[8]{0:T(128)}, f32[8]{0:T(128)}, f32[8,16,16,128]{3,2,1,0:T(8,128)S(1)}) fusion(f32[8,16,16,128]{3,2,1,0:T(8,128)S(1)} %reshape.119, f32[8,16,16,128]{3,2,1,0:T(8,128)S(1)} %copy-done.1, f32[16,16,128]{2,1,0:T(8,128)S(1)} %mul.300, f32[8,18,1,128]{3,2,1,0:T(1,128)} %copy-done.33, f32[8,18,16,128]{3,2,1,0:T(8,128)} %copy-done.7, ...), kind=kLoop, calls=%fused_computation.104 | loop fusion | flops 8912880 | bytes 5673280 | tf_op jit(solution)/shard_map/reduce_sum | solution.py:45
  138.4 42.6 %all-reduce.1 = (f32[8]{0:T(128)}, f32[8]{0:T(128)}) all-reduce(f32[8]{0:T(128)} %get-tuple-element.10, f32[8]{0:T(128)} %get-tuple-element.9), channel_id=1, replica_groups=mesh['span'=2,'height'=4,'depth'=4] {'span','height','depth'}, use_global_device_ids=true, to_apply=%region_3.4 | all-reduce | flops 16 | bytes 128 | tf_op jit(solution)/shard_map/psum | solution.py:49
  183.2 11.9 %reshape.121 = bf16[8,2,8,2,8,16,8]{6,5,4,3,2,1,0:T(8,128)(2,1)} reshape(bf16[8,16,16,128]{3,2,1,0:T(8,128)(2,1)} %fusion.87) | data formatting | bytes 1048576 | tf_op jit(solution)/shard_map/reshape | solution.py:97
  195.1 6.2 %bitcast_convert_fusion = bf16[16,8,8,8,8]{0,4,3,2,1:T(8,128)(2,1)S(1)} fusion(bf16[8,2,8,2,8,16,8]{6,5,4,3,2,1,0:T(8,128)(2,1)} %reshape.121, f32[2,2,16]{2,1,0:T(2,128)} %copy-done.41, s32[2,2,16]{2,1,0:T(2,128)} %copy-done.44), kind=kOutput, calls=%fused_computation.2 | convolution fusion | flops 8456192 | bytes 655872 | tf_op jit(solution)/shard_map/sxyz,lxiyjzk->slijk/dot_general | solution.py:100
  201.7 5.5 %all_to_all.20 = bf16[16,8,512]{2,1,0:T(8,128)(2,1)S(1)} all-to-all(bf16[16,8,512]{2,1,0:T(8,128)(2,1)S(1)} %copy.31), channel_id=1, replica_groups=mesh['span'=2,'height'=4,'depth'=4] {'span'}, dimensions={0} | all-to-all | bytes 262144 | tf_op jit(solution)/shard_map/all_to_all | solution.py:105
  207.3 5.6 %fusion.124 = f32[16,8,512]{2,1,0:T(8,128)S(1)} fusion(bf16[16,8,512]{2,1,0:T(8,128)(2,1)S(1)} %all_to_all.20, bf16[16,512,512]{2,1,0:T(8,128)(2,1)} %param.9), kind=kOutput, calls=%fused_computation.251 | convolution fusion | flops 67108864 | bytes 8781824 | tf_op jit(solution)/shard_map/sij,slj->sli/dot_general | solution.py:93
  212.9 7.7 %all_to_all.21 = f32[16,8,512]{2,1,0:T(8,128)S(1)} all-to-all(f32[16,8,512]{2,1,0:T(8,128)S(1)} %fusion.124), channel_id=1, replica_groups=mesh['span'=2,'height'=4,'depth'=4] {'span'}, dimensions={0} | all-to-all | bytes 524288 | tf_op jit(solution)/shard_map/all_to_all | solution.py:94
  222.5 10.1 %convolution_bitcast_fusion = f32[8,2,8,2,8,16,8]{5,6,3,1,4,2,0:T(8,128)} fusion(f32[16,8,8,8,8,1,1]{0,4,6,5,3,2,1:T(8,128)} %bitcast.147, f32[2,2,16]{2,1,0:T(2,128)S(1)} %copy-done.43, s32[2,2,16]{2,1,0:T(2,128)S(1)} %copy-done.45), kind=kOutput, calls=%fused_computation | convolution fusion | flops 50333696 | bytes 1311232 | tf_op jit(solution)/shard_map/sxyz,slijk->lxiyjzk/dot_general | solution.py:108
  232.6 12.3 %copy.33 = f32[8,2,8,2,8,16,8]{6,5,4,3,2,1,0:T(8,128)} copy(f32[8,2,8,2,8,16,8]{5,6,3,1,4,2,0:T(8,128)} %convolution_bitcast_fusion) | data formatting | bytes 2097152 | tf_op jit(solution)/shard_map/sxyz,slijk->lxiyjzk/transpose | solution.py:108
  244.9 11.9 %reshape.124 = f32[8,16,16,128]{3,2,1,0:T(8,128)S(1)} reshape(f32[8,2,8,2,8,16,8]{6,5,4,3,2,1,0:T(8,128)} %copy.33) | data formatting | bytes 2097152 | tf_op jit(solution)/shard_map/reshape | solution.py:111
  258.8 4.5 collective-permute-start.25
  264.7 4.8 %collective-permute-start.12 = (f32[8,1,16,128]{3,2,1,0:T(8,128)S(1)}, f32[8,1,16,128]{3,2,1,0:T(8,128)S(1)}, u32[]{:S(2)}, u32[]{:S(2)}) collective-permute-start(f32[8,1,16,128]{3,2,1,0:T(8,128)S(1)} %get-tuple-element.34), channel_id=1, source_target_pairs={{16,0},{17,1},{18,2},{19,3},{20,4},{21,5},{22,6},{23,7},{24,8},{25... | collective-permute-start | bytes 196616 | tf_op jit(solution)/shard_map/ppermute | solution.py:24
  276.8 3.2 collective-permute-start.27
  285.3 3.1 copy.36
  288.3 3.3 collective-permute-start.17
  291.6 3.0 copy.34
  294.6 3.2 collective-permute-start.16
  298.6 3.1 copy.37
  301.8 3.1 copy.35
  304.9 5.0 %fusion.22 = f32[8]{0:T(128)S(1)} fusion(f32[8,16,16,128]{3,2,1,0:T(8,128)S(1)} %reshape.124, f32[8,18,18,1]{3,2,1,0:T(8,128)} %copy.37, f32[8,18,1,128]{3,2,1,0:T(1,128)S(1)} %collective-permute-done.14, f32[8,18,16,128]{3,2,1,0:T(8,128)} %copy-done.8, f32[8,18,1,128]{3,2,1,0:T(1,128)} %copy-done.35, f32[8,18,18,1]{3,2,1,0:T(8,128)} %copy.35, ...), kind=kLoop, calls=%fused_computation.48 | loop fusion | flops 8126456 | bytes 3445024 | tf_op jit(solution)/shard_map/reduce_sum | solution.py:45
  310.0 39.8 %all-reduce = (f32[8]{0:T(128)S(1)}, f32[8]{0:T(128)S(1)}) all-reduce(f32[8]{0:T(128)S(1)} %copy-done.59, f32[8]{0:T(128)S(1)} %fusion.22), channel_id=1, replica_groups=mesh['span'=2,'height'=4,'depth'=4] {'span','height','depth'}, use_global_device_ids=true, to_apply=%region_7.8 | all-reduce | flops 16 | bytes 128 | tf_op jit(solution)/shard_map/psum | solution.py:49
  350.8 2.9 collective-permute-start.18
  356.1 3.3 collective-permute-start.29
  359.3 2.6 collective-permute-start.28
  371.7 3.0 copy.38
  374.7 3.3 collective-permute-start.22
  379.6 2.6 collective-permute-start.23
  388.2 3.2 fusion.5
  393.5 41.7 %pmax.7 = f32[]{:T(128)} all-reduce(f32[]{:T(128)} %get-tuple-element.15), channel_id=1, replica_groups=mesh['span'=2,'height'=4,'depth'=4] {'span','height','depth'}, use_global_device_ids=true, to_apply=%region_17.18 | all-reduce | flops 1 | bytes 8 | tf_op jit(solution)/shard_map/pmax | solution.py:143
  439.2 4.2 collective-permute-done.30
  447.8 2.6 collective-permute-done.32
  450.5 3.2 collective-permute-start.35
  453.7 2.6 collective-permute-start.34
  457.1 3.2 collective-permute-done.34
  (245 shorter events, 97.9 us)
Async XLA Ops:
  5.8 15.1 %collective-permute-start = (f32[2,1,16,128]{3,2,1,0:T(8,128)S(1)}, f32[2,1,16,128]{3,2,1,0:T(8,128)S(1)}, u32[]{:S(2)}, u32[]{:S(2)}) collective-permute-start(f32[2,1,16,128]{3,2,1,0:T(8,128)S(1)} %get-tuple-element.49), channel_id=1, source_target_pairs={{16,0},{17,1},{18,2},{19,3},{20,4},{21,5},{22,6},{23,7},{24,8},{25... | collective-permute-start | bytes 49160 | tf_op jit(solution)/shard_map/ppermute | solution.py:24
  8.2 12.6 %collective-permute-start.2 = (f32[2,1,16,128]{3,2,1,0:T(8,128)S(1)}, f32[2,1,16,128]{3,2,1,0:T(8,128)S(1)}, u32[]{:S(2)}, u32[]{:S(2)}) collective-permute-start(f32[2,1,16,128]{3,2,1,0:T(8,128)S(1)} %get-tuple-element.48), channel_id=1, source_target_pairs={{0,16},{1,17},{2,18},{3,19},{4,20},{5,21},{6,22},{7,23},{8,24},{9,... | collective-permute-start | bytes 49160 | tf_op jit(solution)/shard_map/ppermute | solution.py:21
  20.8 36.5 %copy-start.21 = (f32[2,1,16,128]{3,2,1,0:T(8,128)}, f32[2,1,16,128]{3,2,1,0:T(8,128)S(1)}, u32[]{:S(2)}) copy-start(f32[2,1,16,128]{3,2,1,0:T(8,128)S(1)} %collective-permute-done.2) | copy-start | bytes 49156
  20.9 17.6 %collective-permute-start.4 = (f32[2,18,1,128]{3,2,1,0:T(1,128)S(1)}, f32[2,18,1,128]{3,2,1,0:T(1,128)S(1)}, u32[]{:S(2)}, u32[]{:S(2)}) collective-permute-start(f32[2,18,1,128]{3,2,1,0:T(1,128)S(1)} %get-tuple-element.47), channel_id=1, source_target_pairs={{4,0},{8,4},{12,8},{5,1},{9,5},{13,9},{6,2},{10,6},{14,10},{7,3},{... | collective-permute-start | bytes 55304 | tf_op jit(solution)/shard_map/ppermute | solution.py:24
  22.8 15.7 %collective-permute-start.6 = (f32[2,18,1,128]{3,2,1,0:T(1,128)S(1)}, f32[2,18,1,128]{3,2,1,0:T(1,128)S(1)}, u32[]{:S(2)}, u32[]{:S(2)}) collective-permute-start(f32[2,18,1,128]{3,2,1,0:T(1,128)S(1)} %get-tuple-element.46), channel_id=1, source_target_pairs={{0,4},{4,8},{8,12},{1,5},{5,9},{9,13},{2,6},{6,10},{10,14},{3,7},{... | collective-permute-start | bytes 55304 | tf_op jit(solution)/shard_map/ppermute | solution.py:21
  32.5 13.9 %all-to-all-start = ((bf16[16,8,512]{2,1,0:T(8,128)(2,1)}), bf16[16,8,512]{2,1,0:T(8,128)(2,1)S(1)}, u32[]{:S(2)}, u32[]{:S(2)}) async-start(bf16[16,8,512]{2,1,0:T(8,128)(2,1)} %copy.23), calls=%async_computation | async-start | bytes 262144 | tf_op jit(solution)/shard_map/all_to_all | solution.py:105
  38.5 18.8 %copy-start.30 = (f32[2,18,1,128]{3,2,1,0:T(1,128)}, f32[2,18,1,128]{3,2,1,0:T(1,128)S(1)}, u32[]{:S(2)}) copy-start(f32[2,18,1,128]{3,2,1,0:T(1,128)S(1)} %collective-permute-done.6) | copy-start | bytes 55300
  39.6 69.8 %collective-permute-start.10 = (f32[2,18,18,1]{3,2,1,0:T(8,128)}, f32[2,18,18,1]{3,2,1,0:T(8,128)}, u32[]{:S(2)}, u32[]{:S(2)}) collective-permute-start(f32[2,18,18,1]{3,2,1,0:T(8,128)} %get-tuple-element.45), channel_id=1, source_target_pairs={{0,1},{1,2},{2,3},{4,5},{5,6},{6,7},{8,9},{9,10},{10,11},{12,13},{... | collective-permute-start | bytes 7784 | tf_op jit(solution)/shard_map/ppermute | solution.py:21
  43.1 83.1 %collective-permute-start.8 = (f32[2,18,18,1]{3,2,1,0:T(8,128)}, f32[2,18,18,1]{3,2,1,0:T(8,128)}, u32[]{:S(2)}, u32[]{:S(2)}) collective-permute-start(f32[2,18,18,1]{3,2,1,0:T(8,128)} %get-tuple-element.44), channel_id=1, source_target_pairs={{1,0},{2,1},{3,2},{5,4},{6,5},{7,6},{9,8},{10,9},{11,10},{13,12},{... | collective-permute-start | bytes 7784 | tf_op jit(solution)/shard_map/ppermute | solution.py:24
  52.7 7.9 %all-to-all-start.1 = ((f32[16,8,512]{2,1,0:T(8,128)}), f32[16,8,512]{2,1,0:T(8,128)}, u32[]{:S(2)}, u32[]{:S(2)}) async-start(f32[16,8,512]{2,1,0:T(8,128)} %fusion.123), calls=%async_computation.1 | async-start | bytes 524288 | tf_op jit(solution)/shard_map/all_to_all | solution.py:94
  95.9 6.7 %collective-permute-start.3 = (f32[8,1,16,128]{3,2,1,0:T(8,128)S(1)}, f32[8,1,16,128]{3,2,1,0:T(8,128)S(1)}, u32[]{:S(2)}, u32[]{:S(2)}) collective-permute-start(f32[8,1,16,128]{3,2,1,0:T(8,128)S(1)} %get-tuple-element.39), channel_id=1, source_target_pairs={{0,16},{1,17},{2,18},{3,19},{4,20},{5,21},{6,22},{7,23},{8,24},{9,... | collective-permute-start | bytes 196616 | tf_op jit(solution)/shard_map/ppermute | solution.py:21
  98.0 6.4 %collective-permute-start.1 = (f32[8,1,16,128]{3,2,1,0:T(8,128)S(1)}, f32[8,1,16,128]{3,2,1,0:T(8,128)S(1)}, u32[]{:S(2)}, u32[]{:S(2)}) collective-permute-start(f32[8,1,16,128]{3,2,1,0:T(8,128)S(1)} %get-tuple-element.38), channel_id=1, source_target_pairs={{16,0},{17,1},{18,2},{19,3},{20,4},{21,5},{22,6},{23,7},{24,8},{25... | collective-permute-start | bytes 196616 | tf_op jit(solution)/shard_map/ppermute | solution.py:24
  105.0 6.2 %collective-permute-start.5 = (f32[8,18,1,128]{3,2,1,0:T(1,128)S(1)}, f32[8,18,1,128]{3,2,1,0:T(1,128)S(1)}, u32[]{:S(2)}, u32[]{:S(2)}) collective-permute-start(f32[8,18,1,128]{3,2,1,0:T(1,128)S(1)} %get-tuple-element.31), channel_id=1, source_target_pairs={{4,0},{8,4},{12,8},{5,1},{9,5},{13,9},{6,2},{10,6},{14,10},{7,3},{... | collective-permute-start | bytes 221192 | tf_op jit(solution)/shard_map/ppermute | solution.py:24
  107.2 5.7 %collective-permute-start.7 = (f32[8,18,1,128]{3,2,1,0:T(1,128)S(1)}, f32[8,18,1,128]{3,2,1,0:T(1,128)S(1)}, u32[]{:S(2)}, u32[]{:S(2)}) collective-permute-start(f32[8,18,1,128]{3,2,1,0:T(1,128)S(1)} %get-tuple-element.30), channel_id=1, source_target_pairs={{0,4},{4,8},{8,12},{1,5},{5,9},{9,13},{2,6},{6,10},{10,14},{3,7},{... | collective-permute-start | bytes 221192 | tf_op jit(solution)/shard_map/ppermute | solution.py:21
  117.9 10.2 %collective-permute-start.11 = (f32[8,18,18,1]{2,0,3,1:T(8,128)S(1)}, f32[8,18,18,1]{2,0,3,1:T(8,128)S(1)}, u32[]{:S(2)}, u32[]{:S(2)}) collective-permute-start(f32[8,18,18,1]{2,0,3,1:T(8,128)S(1)} %copy.28), channel_id=1, source_target_pairs={{0,1},{1,2},{2,3},{4,5},{5,6},{6,7},{8,9},{9,10},{10,11},{12,13},{... | collective-permute-start | bytes 31112 | tf_op jit(solution)/shard_map/ppermute | solution.py:21
  123.1 7.2 %collective-permute-start.9 = (f32[8,18,18,1]{2,0,3,1:T(8,128)S(1)}, f32[8,18,18,1]{2,0,3,1:T(8,128)S(1)}, u32[]{:S(2)}, u32[]{:S(2)}) collective-permute-start(f32[8,18,18,1]{2,0,3,1:T(8,128)S(1)} %copy.26), channel_id=1, source_target_pairs={{1,0},{2,1},{3,2},{5,4},{6,5},{7,6},{9,8},{10,9},{11,10},{13,12},{... | collective-permute-start | bytes 31112 | tf_op jit(solution)/shard_map/ppermute | solution.py:24
  138.4 56.8 %copy-start.3 = (f32[8,16,16,128]{3,2,1,0:T(8,128)}, f32[8,16,16,128]{3,2,1,0:T(8,128)S(1)}, u32[]{:S(2)}) copy-start(f32[8,16,16,128]{3,2,1,0:T(8,128)S(1)} %get-tuple-element.19) | copy-start | bytes 3145732
  244.9 25.1 %copy-start.2 = (f32[8,16,16,128]{3,2,1,0:T(8,128)S(1)}, f32[8,16,16,128]{3,2,1,0:T(8,128)}, u32[]{:S(2)}) copy-start(f32[8,16,16,128]{3,2,1,0:T(8,128)} %param.5) | copy-start | bytes 3145732
  256.8 12.6 %collective-permute-start.13 = (f32[8,1,16,128]{3,2,1,0:T(8,128)S(1)}, f32[8,1,16,128]{3,2,1,0:T(8,128)S(1)}, u32[]{:S(2)}, u32[]{:S(2)}) collective-permute-start(f32[8,1,16,128]{3,2,1,0:T(8,128)S(1)} %get-tuple-element.35), channel_id=1, source_target_pairs={{0,16},{1,17},{2,18},{3,19},{4,20},{5,21},{6,22},{7,23},{8,24},{9,... | collective-permute-start | bytes 196616 | tf_op jit(solution)/shard_map/ppermute | solution.py:21
  258.8 17.9 %collective-permute-start.25 = (bf16[1,16,128]{2,1,0:T(8,128)(2,1)S(1)}, bf16[1,16,128]{2,1,0:T(8,128)(2,1)S(1)}, u32[]{:S(2)}, u32[]{:S(2)}) collective-permute-start(bf16[1,16,128]{2,1,0:T(8,128)(2,1)S(1)} %get-tuple-element.63), channel_id=1, source_target_pairs={{16,0},{17,1},{18,2},{19,3},{20,4},{21,5},{22,6},{23,7},{24,8},{25... | collective-permute-start | bytes 12296 | tf_op jit(solution)/shard_map/ppermute | solution.py:24
  263.4 13.4 %collective-permute-start.24 = (bf16[1,16,128]{2,1,0:T(8,128)(2,1)S(1)}, bf16[1,16,128]{2,1,0:T(8,128)(2,1)S(1)}, u32[]{:S(2)}, u32[]{:S(2)}) collective-permute-start(bf16[1,16,128]{2,1,0:T(8,128)(2,1)S(1)} %get-tuple-element.62), channel_id=1, source_target_pairs={{0,16},{1,17},{2,18},{3,19},{4,20},{5,21},{6,22},{7,23},{8,24},{9,... | collective-permute-start | bytes 12296 | tf_op jit(solution)/shard_map/ppermute | solution.py:21
  264.7 7.6 %collective-permute-start.12 = (f32[8,1,16,128]{3,2,1,0:T(8,128)S(1)}, f32[8,1,16,128]{3,2,1,0:T(8,128)S(1)}, u32[]{:S(2)}, u32[]{:S(2)}) collective-permute-start(f32[8,1,16,128]{3,2,1,0:T(8,128)S(1)} %get-tuple-element.34), channel_id=1, source_target_pairs={{16,0},{17,1},{18,2},{19,3},{20,4},{21,5},{22,6},{23,7},{24,8},{25... | collective-permute-start | bytes 196616 | tf_op jit(solution)/shard_map/ppermute | solution.py:24
  272.4 9.5 %collective-permute-start.14 = (f32[8,18,1,128]{3,2,1,0:T(1,128)S(1)}, f32[8,18,1,128]{3,2,1,0:T(1,128)S(1)}, u32[]{:S(2)}, u32[]{:S(2)}) collective-permute-start(f32[8,18,1,128]{3,2,1,0:T(1,128)S(1)} %get-tuple-element.29), channel_id=1, source_target_pairs={{4,0},{8,4},{12,8},{5,1},{9,5},{13,9},{6,2},{10,6},{14,10},{7,3},{... | collective-permute-start | bytes 221192 | tf_op jit(solution)/shard_map/ppermute | solution.py:24
  274.3 7.6 %collective-permute-start.15 = (f32[8,18,1,128]{3,2,1,0:T(1,128)S(1)}, f32[8,18,1,128]{3,2,1,0:T(1,128)S(1)}, u32[]{:S(2)}, u32[]{:S(2)}) collective-permute-start(f32[8,18,1,128]{3,2,1,0:T(1,128)S(1)} %get-tuple-element.28), channel_id=1, source_target_pairs={{0,4},{4,8},{8,12},{1,5},{5,9},{9,13},{2,6},{6,10},{10,14},{3,7},{... | collective-permute-start | bytes 221192 | tf_op jit(solution)/shard_map/ppermute | solution.py:21
  276.8 21.0 %collective-permute-start.27 = (bf16[18,1,128]{2,1,0:T(2,128)(2,1)S(1)}, bf16[18,1,128]{2,1,0:T(2,128)(2,1)S(1)}, u32[]{:S(2)}, u32[]{:S(2)}) collective-permute-start(bf16[18,1,128]{2,1,0:T(2,128)(2,1)S(1)} %get-tuple-element.59), channel_id=1, source_target_pairs={{4,0},{8,4},{12,8},{5,1},{9,5},{13,9},{6,2},{10,6},{14,10},{7,3},{... | collective-permute-start | bytes 13832 | tf_op jit(solution)/shard_map/ppermute | solution.py:24
  280.0 17.9 %collective-permute-start.26 = (bf16[18,1,128]{2,1,0:T(2,128)(2,1)S(1)}, bf16[18,1,128]{2,1,0:T(2,128)(2,1)S(1)}, u32[]{:S(2)}, u32[]{:S(2)}) collective-permute-start(bf16[18,1,128]{2,1,0:T(2,128)(2,1)S(1)} %get-tuple-element.58), channel_id=1, source_target_pairs={{0,4},{4,8},{8,12},{1,5},{5,9},{9,13},{2,6},{6,10},{10,14},{3,7},{... | collective-permute-start | bytes 13832 | tf_op jit(solution)/shard_map/ppermute | solution.py:21
  288.3 10.3 %collective-permute-start.17 = (f32[8,18,18,1]{2,0,3,1:T(8,128)}, f32[8,18,18,1]{2,0,3,1:T(8,128)}, u32[]{:S(2)}, u32[]{:S(2)}) collective-permute-start(f32[8,18,18,1]{2,0,3,1:T(8,128)} %copy.36), channel_id=1, source_target_pairs={{0,1},{1,2},{2,3},{4,5},{5,6},{6,7},{8,9},{9,10},{10,11},{12,13},{... | collective-permute-start | bytes 31112 | tf_op jit(solution)/shard_map/ppermute | solution.py:21
  294.6 7.1 %collective-permute-start.16 = (f32[8,18,18,1]{2,0,3,1:T(8,128)}, f32[8,18,18,1]{2,0,3,1:T(8,128)}, u32[]{:S(2)}, u32[]{:S(2)}) collective-permute-start(f32[8,18,18,1]{2,0,3,1:T(8,128)} %copy.34), channel_id=1, source_target_pairs={{1,0},{2,1},{3,2},{5,4},{6,5},{7,6},{9,8},{10,9},{11,10},{13,12},{... | collective-permute-start | bytes 31112 | tf_op jit(solution)/shard_map/ppermute | solution.py:24
  304.9 44.9 %copy-start.60 = (f32[8]{0:T(128)S(1)}, f32[8]{0:T(128)}, u32[]{:S(2)}) copy-start(f32[8]{0:T(128)} %get-tuple-element.13) | copy-start | bytes 100
  304.9 44.9 %copy-start.61 = (f32[8]{0:T(128)S(1)}, f32[8]{0:T(128)}, u32[]{:S(2)}) copy-start(f32[8]{0:T(128)} %get-tuple-element.14) | copy-start | bytes 100
  350.7 37.5 %copy-start = (f32[8,16,16,128]{3,2,1,0:T(8,128)}, f32[8,16,16,128]{3,2,1,0:T(8,128)S(1)}, u32[]{:S(2)}) copy-start(f32[8,16,16,128]{3,2,1,0:T(8,128)S(1)} %multiply_add_fusion) | copy-start | bytes 3145732
  350.7 15.7 %copy-start.20 = (bf16[16,16,128]{2,1,0:T(8,128)(2,1)S(1)}, bf16[16,16,128]{2,1,0:T(8,128)(2,1)}, u32[]{:S(2)}) copy-start(bf16[16,16,128]{2,1,0:T(8,128)(2,1)} %get-tuple-element.50) | copy-start | bytes 196612
  350.8 11.1 %collective-permute-start.18 = (f32[8,1,16,128]{3,2,1,0:T(8,128)S(1)}, f32[8,1,16,128]{3,2,1,0:T(8,128)S(1)}, u32[]{:S(2)}, u32[]{:S(2)}) collective-permute-start(f32[8,1,16,128]{3,2,1,0:T(8,128)S(1)} %get-tuple-element.33), channel_id=1, source_target_pairs={{16,0},{17,1},{18,2},{19,3},{20,4},{21,5},{22,6},{23,7},{24,8},{25... | collective-permute-start | bytes 196616 | tf_op jit(solution)/shard_map/ppermute | solution.py:24
  353.7 8.2 %collective-permute-start.19 = (f32[8,1,16,128]{3,2,1,0:T(8,128)S(1)}, f32[8,1,16,128]{3,2,1,0:T(8,128)S(1)}, u32[]{:S(2)}, u32[]{:S(2)}) collective-permute-start(f32[8,1,16,128]{3,2,1,0:T(8,128)S(1)} %get-tuple-element.32), channel_id=1, source_target_pairs={{0,16},{1,17},{2,18},{3,19},{4,20},{5,21},{6,22},{7,23},{8,24},{9,... | collective-permute-start | bytes 196616 | tf_op jit(solution)/shard_map/ppermute | solution.py:21
  356.1 10.3 %collective-permute-start.29 = (bf16[18,18,1]{2,1,0:T(8,128)(2,1)S(1)}, bf16[18,18,1]{2,1,0:T(8,128)(2,1)S(1)}, u32[]{:S(2)}, u32[]{:S(2)}) collective-permute-start(bf16[18,18,1]{2,1,0:T(8,128)(2,1)S(1)} %get-tuple-element.55), channel_id=1, source_target_pairs={{1,0},{2,1},{3,2},{5,4},{6,5},{7,6},{9,8},{10,9},{11,10},{13,12},{... | collective-permute-start | bytes 1952 | tf_op jit(solution)/shard_map/ppermute | solution.py:24
  359.3 7.1 %collective-permute-start.28 = (bf16[18,18,1]{2,1,0:T(8,128)(2,1)S(1)}, bf16[18,18,1]{2,1,0:T(8,128)(2,1)S(1)}, u32[]{:S(2)}, u32[]{:S(2)}) collective-permute-start(bf16[18,18,1]{2,1,0:T(8,128)(2,1)S(1)} %get-tuple-element.54), channel_id=1, source_target_pairs={{0,1},{1,2},{2,3},{4,5},{5,6},{6,7},{8,9},{9,10},{10,11},{12,13},{... | collective-permute-start | bytes 1952 | tf_op jit(solution)/shard_map/ppermute | solution.py:21
  362.1 5.4 %collective-permute-start.20 = (f32[8,18,1,128]{3,2,1,0:T(1,128)S(1)}, f32[8,18,1,128]{3,2,1,0:T(1,128)S(1)}, u32[]{:S(2)}, u32[]{:S(2)}) collective-permute-start(f32[8,18,1,128]{3,2,1,0:T(1,128)S(1)} %get-tuple-element.27), channel_id=1, source_target_pairs={{4,0},{8,4},{12,8},{5,1},{9,5},{13,9},{6,2},{10,6},{14,10},{7,3},{... | collective-permute-start | bytes 221192 | tf_op jit(solution)/shard_map/ppermute | solution.py:24
  364.0 5.7 %collective-permute-start.21 = (f32[8,18,1,128]{3,2,1,0:T(1,128)S(1)}, f32[8,18,1,128]{3,2,1,0:T(1,128)S(1)}, u32[]{:S(2)}, u32[]{:S(2)}) collective-permute-start(f32[8,18,1,128]{3,2,1,0:T(1,128)S(1)} %get-tuple-element.26), channel_id=1, source_target_pairs={{0,4},{4,8},{8,12},{1,5},{5,9},{9,13},{2,6},{6,10},{10,14},{3,7},{... | collective-permute-start | bytes 221192 | tf_op jit(solution)/shard_map/ppermute | solution.py:21
  374.7 8.4 %collective-permute-start.22 = (f32[8,18,18,1]{2,0,3,1:T(8,128)}, f32[8,18,18,1]{2,0,3,1:T(8,128)}, u32[]{:S(2)}, u32[]{:S(2)}) collective-permute-start(f32[8,18,18,1]{2,0,3,1:T(8,128)} %copy.38), channel_id=1, source_target_pairs={{1,0},{2,1},{3,2},{5,4},{6,5},{7,6},{9,8},{10,9},{11,10},{13,12},{... | collective-permute-start | bytes 31112 | tf_op jit(solution)/shard_map/ppermute | solution.py:24
  379.6 6.4 %collective-permute-start.23 = (f32[8,18,18,1]{2,0,3,1:T(8,128)}, f32[8,18,18,1]{2,0,3,1:T(8,128)S(1)}, u32[]{:S(2)}, u32[]{:S(2)}) collective-permute-start(f32[8,18,18,1]{2,0,3,1:T(8,128)} %copy.40), channel_id=1, source_target_pairs={{0,1},{1,2},{2,3},{4,5},{5,6},{6,7},{8,9},{9,10},{10,11},{12,13},{... | collective-permute-start | bytes 31112 | tf_op jit(solution)/shard_map/ppermute | solution.py:21
  391.5 44.4 %copy-start.9 = (f32[18,18,130]{2,1,0:T(8,128)S(1)}, f32[18,18,130]{2,1,0:T(8,128)}, u32[]{:S(2)}) copy-start(f32[18,18,130]{2,1,0:T(8,128)} %maximum_convert_fusion) | copy-start | bytes 505444
  393.5 68.0 %copy-start.17 = (f32[16,16,128]{2,1,0:T(8,128)}, f32[16,16,128]{2,1,0:T(8,128)S(1)}, u32[]{:S(2)}) copy-start(f32[16,16,128]{2,1,0:T(8,128)S(1)} %get-tuple-element.16) | copy-start | bytes 393220
  436.1 3.1 collective-permute-start.31
  437.9 5.5 %collective-permute-start.30 = (bf16[1,16,128]{2,1,0:T(8,128)(2,1)S(1)}, bf16[1,16,128]{2,1,0:T(8,128)(2,1)S(1)}, u32[]{:S(2)}, u32[]{:S(2)}) collective-permute-start(bf16[1,16,128]{2,1,0:T(8,128)(2,1)S(1)} %get-tuple-element.60), channel_id=1, source_target_pairs={{0,16},{1,17},{2,18},{3,19},{4,20},{5,21},{6,22},{7,23},{8,24},{9,... | collective-permute-start | bytes 12296 | tf_op jit(solution)/shard_map/ppermute | solution.py:21
  443.4 4.3 collective-permute-start.33
  445.3 5.0 %collective-permute-start.32 = (bf16[18,1,128]{2,1,0:T(2,128)(2,1)S(1)}, bf16[18,1,128]{2,1,0:T(2,128)(2,1)S(1)}, u32[]{:S(2)}, u32[]{:S(2)}) collective-permute-start(bf16[18,1,128]{2,1,0:T(2,128)(2,1)S(1)} %get-tuple-element.56), channel_id=1, source_target_pairs={{0,4},{4,8},{8,12},{1,5},{5,9},{9,13},{2,6},{6,10},{10,14},{3,7},{... | collective-permute-start | bytes 13832 | tf_op jit(solution)/shard_map/ppermute | solution.py:21
  450.5 6.6 %collective-permute-start.35 = (bf16[18,18,1]{2,1,0:T(8,128)(2,1)S(1)}, bf16[18,18,1]{2,1,0:T(8,128)(2,1)S(1)}, u32[]{:S(2)}, u32[]{:S(2)}) collective-permute-start(bf16[18,18,1]{2,1,0:T(8,128)(2,1)S(1)} %get-tuple-element.53), channel_id=1, source_target_pairs={{1,0},{2,1},{3,2},{5,4},{6,5},{7,6},{9,8},{10,9},{11,10},{13,12},{... | collective-permute-start | bytes 1952 | tf_op jit(solution)/shard_map/ppermute | solution.py:24
  453.7 6.6 %collective-permute-start.34 = (bf16[18,18,1]{2,1,0:T(8,128)(2,1)S(1)}, bf16[18,18,1]{2,1,0:T(8,128)(2,1)S(1)}, u32[]{:S(2)}, u32[]{:S(2)}) collective-permute-start(bf16[18,18,1]{2,1,0:T(8,128)(2,1)S(1)} %get-tuple-element.52), channel_id=1, source_target_pairs={{0,1},{1,2},{2,3},{4,5},{5,6},{6,7},{8,9},{9,10},{10,11},{12,13},{... | collective-permute-start | bytes 1952 | tf_op jit(solution)/shard_map/ppermute | solution.py:21
  (52 other events, 401.0 us)
where the time goes:
time: 471 us; the launch traced here: 462 us
  blocking collectives  137 us (29%)
  local copies, waits for them, and re-layouts  121 us (26%)
  starting transfers between devices  102 us (22%)
  matrix products  44 us (9%)
  other arithmetic  34.2 us (7%)
  waiting for transfers between devices  19.7 us (4%)
    psum x2, blocking collectives, paired_sums(): lax.psum((cell_sums(residual, search), cell_sums(image, search)), ('span'...  82.4 us
    ppermute x18, starting transfers between devices, padded_2(): lax.ppermute(lax.slice_in_dim(block, 0, width, axis=dim), axis, backward)  53.1 us
    pmax x1, blocking collectives, local(): peak_value = lax.pmax(jnp.max(-sensitivity), ('span', 'height', 'depth'))  41.7 us
    ppermute x18, starting transfers between devices, padded_2(): lax.ppermute(lax.slice_in_dim(block, block.shape[dim] - width, None, axis...  38.7 us
    transpose x2, local copies, waits for them, and re-layouts, precondition(): jnp.einsum('sxyz,slijk->lxiyjzk', selector, shaped, precision=lax.Precisi...  24.7 us
    reshape x2, local copies, waits for them, and re-layouts, precondition(): return placed.reshape(loads, extents[0], extents[1], extents[2])  23.7 us
    reshape x2, local copies, waits for them, and re-layouts, precondition(): residual.astype(jnp.bfloat16)  22.5 us
    dot_general x2, matrix products, precondition(): jnp.einsum('sxyz,slijk->lxiyjzk', selector, shaped, precision=lax.Precisi...  19.6 us
  transfers between devices with their start and end apart: 38, of which 9 were waited for; matrix products, arithmetic and copies ran while one was open for 21% of the time, Pallas kernels for 0%

commit v1 on v0

--- a/solution.py
+++ b/solution.py
@@ -47,7 +47,8 @@
 
 def paired_sums(residual, search, image):
     return lax.psum(
-        (cell_sums(residual, search), cell_sums(image, search)), ("span", "height", "depth")
+        lax.psum((cell_sums(residual, search), cell_sums(image, search)), "span"),
+        ("height", "depth"),
     )
 
 

time: 471 us -> 462 us (0.981)
  blocking collectives: 137 us -> 128 us
    psum x2 -> x4, blocking collectives: 82.4 us -> 72.3 us  [the longest x2 61.5 us: paired_sums(): lax.psum(lax.psum((cell_sums(residual, search), cell_sums(image, search))...]
  transfers between devices with their start and end apart: 38 -> 38, of which waited for: 9 -> 9; matrix products, arithmetic and copies ran while one was open for 21% -> 22% of each run, Pallas kernels for 0% -> 0%
where the time goes in v1:
time: 462 us; the launch traced here: 453 us
  blocking collectives  128 us (28%)
  local copies, waits for them, and re-layouts  121 us (26%)
  starting transfers between devices  103 us (22%)
  matrix products  44 us (10%)
  other arithmetic  34.2 us (7%)
  waiting for transfers between devices  19.8 us (4%)
    psum x2, blocking collectives, paired_sums(): lax.psum(lax.psum((cell_sums(residual, search), cell_sums(image, search))...  61.5 us
    ppermute x18, starting transfers between devices, padded_2(): lax.ppermute(lax.slice_in_dim(block, 0, width, axis=dim), axis, backward)  54.5 us
    pmax x1, blocking collectives, local(): peak_value = lax.pmax(jnp.max(-sensitivity), ('span', 'height', 'depth'))  41.3 us
    ppermute x18, starting transfers between devices, padded_2(): lax.ppermute(lax.slice_in_dim(block, block.shape[dim] - width, None, axis...  37.8 us
    transpose x2, local copies, waits for them, and re-layouts, precondition(): jnp.einsum('sxyz,slijk->lxiyjzk', selector, shaped, precision=lax.Precisi...  24.7 us
    reshape x2, local copies, waits for them, and re-layouts, precondition(): return placed.reshape(loads, extents[0], extents[1], extents[2])  23.7 us
    reshape x2, local copies, waits for them, and re-layouts, precondition(): residual.astype(jnp.bfloat16)  22.5 us
    dot_general x2, matrix products, precondition(): jnp.einsum('sxyz,slijk->lxiyjzk', selector, shaped, precision=lax.Precisi...  19.6 us
  transfers between devices with their start and end apart: 38, of which 9 were waited for; matrix products, arithmetic and copies ran while one was open for 22% of the time, Pallas kernels for 0%

profile of v1, /device:TPU:14, one launch (start us, length us, event | category | flops | bytes accessed | tf_op | source)
XLA Modules:
  0.0 453.2 jit_solution(4310318426741705558)
XLA Ops:
  5.8 2.4 collective-permute-start
  10.2 10.6 %reshape.116 = bf16[8,2,8,2,8,16,8]{6,5,4,3,2,1,0:T(8,128)(2,1)} reshape(bf16[8,16,16,128]{3,2,1,0:T(8,128)(2,1)S(1)} %multiply_convert_fusion) | data formatting | bytes 1048576 | tf_op jit(solution)/shard_map/reshape | solution.py:98
  25.2 6.2 %bitcast_convert_fusion.1 = bf16[16,8,8,8,8]{0,4,3,2,1:T(8,128)(2,1)S(1)} fusion(bf16[8,2,8,2,8,16,8]{6,5,4,3,2,1,0:T(8,128)(2,1)} %reshape.116, f32[2,2,16]{2,1,0:T(2,128)S(1)} %copy-done.42, s32[2,2,16]{2,1,0:T(2,128)S(1)} %multiply_add_fusion.1), kind=kOutput, calls=%fused_computation.3 | convolution fusion | flops 8456192 | bytes 655872 | tf_op jit(solution)/shard_map/sxyz,lxiyjzk->slijk/dot_general | solution.py:101
  32.5 6.0 %all-to-all-start = ((bf16[16,8,512]{2,1,0:T(8,128)(2,1)}), bf16[16,8,512]{2,1,0:T(8,128)(2,1)S(1)}, u32[]{:S(2)}, u32[]{:S(2)}) async-start(bf16[16,8,512]{2,1,0:T(8,128)(2,1)} %copy.23), calls=%async_computation | async-start | bytes 262144 | tf_op jit(solution)/shard_map/all_to_all | solution.py:106
  39.6 3.5 collective-permute-start.10
  43.1 3.2 collective-permute-start.8
  46.4 6.4 %fusion.123 = f32[16,8,512]{2,1,0:T(8,128)} fusion(bf16[16,8,512]{2,1,0:T(8,128)(2,1)S(1)} %all-to-all-done, bf16[16,512,512]{2,1,0:T(8,128)(2,1)} %param.9), kind=kOutput, calls=%fused_computation.250 | convolution fusion | flops 67108864 | bytes 8781824 | tf_op jit(solution)/shard_map/sij,slj->sli/dot_general | solution.py:94
  52.7 4.6 %all-to-all-start.1 = ((f32[16,8,512]{2,1,0:T(8,128)}), f32[16,8,512]{2,1,0:T(8,128)}, u32[]{:S(2)}, u32[]{:S(2)}) async-start(f32[16,8,512]{2,1,0:T(8,128)} %fusion.123), calls=%async_computation.1 | async-start | bytes 524288 | tf_op jit(solution)/shard_map/all_to_all | solution.py:95
  62.2 9.5 %convolution_bitcast_fusion.1 = f32[8,2,8,2,8,16,8]{5,6,3,1,4,2,0:T(8,128)} fusion(f32[16,8,8,8,8,1,1]{0,4,6,5,3,2,1:T(8,128)S(1)} %bitcast.148, f32[2,2,16]{2,1,0:T(2,128)} %copy-done.41, s32[2,2,16]{2,1,0:T(2,128)} %copy-done.44), kind=kOutput, calls=%fused_computation.1 | convolution fusion | flops 50333696 | bytes 1311232 | tf_op jit(solution)/shard_map/sxyz,slijk->lxiyjzk/dot_general | solution.py:109
  71.7 12.3 %copy.25 = f32[8,2,8,2,8,16,8]{6,5,4,3,2,1,0:T(8,128)} copy(f32[8,2,8,2,8,16,8]{5,6,3,1,4,2,0:T(8,128)} %convolution_bitcast_fusion.1) | data formatting | bytes 2097152 | tf_op jit(solution)/shard_map/sxyz,slijk->lxiyjzk/transpose | solution.py:109
  84.0 11.8 %reshape.119 = f32[8,16,16,128]{3,2,1,0:T(8,128)S(1)} reshape(f32[8,2,8,2,8,16,8]{6,5,4,3,2,1,0:T(8,128)} %copy.25) | data formatting | bytes 2097152 | tf_op jit(solution)/shard_map/reshape | solution.py:112
  98.0 4.5 %collective-permute-start.1 = (f32[8,1,16,128]{3,2,1,0:T(8,128)S(1)}, f32[8,1,16,128]{3,2,1,0:T(8,128)S(1)}, u32[]{:S(2)}, u32[]{:S(2)}) collective-permute-start(f32[8,1,16,128]{3,2,1,0:T(8,128)S(1)} %get-tuple-element.42), channel_id=1, source_target_pairs={{16,0},{17,1},{18,2},{19,3},{20,4},{21,5},{22,6},{23,7},{24,8},{25... | collective-permute-start | bytes 196616 | tf_op jit(solution)/shard_map/ppermute | solution.py:24
  117.9 2.7 collective-permute-start.11
  123.0 3.1 collective-permute-start.9
  132.5 6.0 %multiply_reduce_fusion.1 = (f32[8]{0:T(128)}, f32[8]{0:T(128)}, f32[8,16,16,128]{3,2,1,0:T(8,128)S(1)}) fusion(f32[8,16,16,128]{3,2,1,0:T(8,128)S(1)} %reshape.119, f32[8,16,16,128]{3,2,1,0:T(8,128)S(1)} %copy-done.1, f32[16,16,128]{2,1,0:T(8,128)S(1)} %mul.300, f32[8,18,1,128]{3,2,1,0:T(1,128)} %copy-done.33, f32[8,18,16,128]{3,2,1,0:T(8,128)} %copy-done.7, ...), kind=kLoop, calls=%fused_computation.104 | loop fusion | flops 8912880 | bytes 5673280 | tf_op jit(solution)/shard_map/reduce_sum | solution.py:45
  138.5 5.8 %all-reduce.3 = (f32[8]{0:T(128)}, f32[8]{0:T(128)}) all-reduce(f32[8]{0:T(128)} %get-tuple-element.10, f32[8]{0:T(128)} %get-tuple-element.9), channel_id=1, replica_groups=mesh['span'=2,'height'=4,'depth'=4] {'span'}, use_global_device_ids=true, to_apply=%region_3.4 | all-reduce | flops 16 | bytes 128 | tf_op jit(solution)/shard_map/psum | solution.py:50
  144.3 30.9 %all-reduce.1 = (f32[8]{0:T(128)}, f32[8]{0:T(128)}) all-reduce(f32[8]{0:T(128)} %get-tuple-element.17, f32[8]{0:T(128)} %get-tuple-element.18), channel_id=1, replica_groups=mesh['span'=2,'height'=4,'depth'=4] {'height','depth'}, use_global_device_ids=true, to_apply=%region_4.5 | all-reduce | flops 16 | bytes 128 | tf_op jit(solution)/shard_map/psum | solution.py:49
  177.4 11.9 %reshape.121 = bf16[8,2,8,2,8,16,8]{6,5,4,3,2,1,0:T(8,128)(2,1)} reshape(bf16[8,16,16,128]{3,2,1,0:T(8,128)(2,1)} %fusion.87) | data formatting | bytes 1048576 | tf_op jit(solution)/shard_map/reshape | solution.py:98
  189.3 6.2 %bitcast_convert_fusion = bf16[16,8,8,8,8]{0,4,3,2,1:T(8,128)(2,1)S(1)} fusion(bf16[8,2,8,2,8,16,8]{6,5,4,3,2,1,0:T(8,128)(2,1)} %reshape.121, f32[2,2,16]{2,1,0:T(2,128)} %copy-done.41, s32[2,2,16]{2,1,0:T(2,128)} %copy-done.44), kind=kOutput, calls=%fused_computation.2 | convolution fusion | flops 8456192 | bytes 655872 | tf_op jit(solution)/shard_map/sxyz,lxiyjzk->slijk/dot_general | solution.py:101
  195.9 6.9 %all_to_all.20 = bf16[16,8,512]{2,1,0:T(8,128)(2,1)S(1)} all-to-all(bf16[16,8,512]{2,1,0:T(8,128)(2,1)S(1)} %copy.31), channel_id=1, replica_groups=mesh['span'=2,'height'=4,'depth'=4] {'span'}, dimensions={0} | all-to-all | bytes 262144 | tf_op jit(solution)/shard_map/all_to_all | solution.py:106
  202.8 5.6 %fusion.124 = f32[16,8,512]{2,1,0:T(8,128)S(1)} fusion(bf16[16,8,512]{2,1,0:T(8,128)(2,1)S(1)} %all_to_all.20, bf16[16,512,512]{2,1,0:T(8,128)(2,1)} %param.9), kind=kOutput, calls=%fused_computation.251 | convolution fusion | flops 67108864 | bytes 8781824 | tf_op jit(solution)/shard_map/sij,slj->sli/dot_general | solution.py:94
  208.4 7.7 %all_to_all.21 = f32[16,8,512]{2,1,0:T(8,128)S(1)} all-to-all(f32[16,8,512]{2,1,0:T(8,128)S(1)} %fusion.124), channel_id=1, replica_groups=mesh['span'=2,'height'=4,'depth'=4] {'span'}, dimensions={0} | all-to-all | bytes 524288 | tf_op jit(solution)/shard_map/all_to_all | solution.py:95
  218.0 10.1 %convolution_bitcast_fusion = f32[8,2,8,2,8,16,8]{5,6,3,1,4,2,0:T(8,128)} fusion(f32[16,8,8,8,8,1,1]{0,4,6,5,3,2,1:T(8,128)} %bitcast.147, f32[2,2,16]{2,1,0:T(2,128)S(1)} %copy-done.43, s32[2,2,16]{2,1,0:T(2,128)S(1)} %copy-done.45), kind=kOutput, calls=%fused_computation | convolution fusion | flops 50333696 | bytes 1311232 | tf_op jit(solution)/shard_map/sxyz,slijk->lxiyjzk/dot_general | solution.py:109
  228.1 12.3 %copy.33 = f32[8,2,8,2,8,16,8]{6,5,4,3,2,1,0:T(8,128)} copy(f32[8,2,8,2,8,16,8]{5,6,3,1,4,2,0:T(8,128)} %convolution_bitcast_fusion) | data formatting | bytes 2097152 | tf_op jit(solution)/shard_map/sxyz,slijk->lxiyjzk/transpose | solution.py:109
  240.4 11.9 %reshape.124 = f32[8,16,16,128]{3,2,1,0:T(8,128)S(1)} reshape(f32[8,2,8,2,8,16,8]{6,5,4,3,2,1,0:T(8,128)} %copy.33) | data formatting | bytes 2097152 | tf_op jit(solution)/shard_map/reshape | solution.py:112
  254.3 4.5 %collective-permute-start.25 = (bf16[1,16,128]{2,1,0:T(8,128)(2,1)S(1)}, bf16[1,16,128]{2,1,0:T(8,128)(2,1)S(1)}, u32[]{:S(2)}, u32[]{:S(2)}) collective-permute-start(bf16[1,16,128]{2,1,0:T(8,128)(2,1)S(1)} %get-tuple-element.67), channel_id=1, source_target_pairs={{16,0},{17,1},{18,2},{19,3},{20,4},{21,5},{22,6},{23,7},{24,8},{25... | collective-permute-start | bytes 12296 | tf_op jit(solution)/shard_map/ppermute | solution.py:24
  260.2 4.5 %collective-permute-start.12 = (f32[8,1,16,128]{3,2,1,0:T(8,128)S(1)}, f32[8,1,16,128]{3,2,1,0:T(8,128)S(1)}, u32[]{:S(2)}, u32[]{:S(2)}) collective-permute-start(f32[8,1,16,128]{3,2,1,0:T(8,128)S(1)} %get-tuple-element.38), channel_id=1, source_target_pairs={{16,0},{17,1},{18,2},{19,3},{20,4},{21,5},{22,6},{23,7},{24,8},{25... | collective-permute-start | bytes 196616 | tf_op jit(solution)/shard_map/ppermute | solution.py:24
  272.1 3.2 collective-permute-start.27
  280.7 3.1 copy.36
  285.7 3.0 copy.34
  288.8 4.5 collective-permute-start.16
  294.1 3.2 copy.37
  297.3 3.1 copy.35
  300.5 5.0 %fusion.22 = f32[8]{0:T(128)S(1)} fusion(f32[8,16,16,128]{3,2,1,0:T(8,128)S(1)} %reshape.124, f32[8,18,18,1]{3,2,1,0:T(8,128)} %copy.37, f32[8,18,1,128]{3,2,1,0:T(1,128)S(1)} %collective-permute-done.14, f32[8,18,16,128]{3,2,1,0:T(8,128)} %copy-done.8, f32[8,18,1,128]{3,2,1,0:T(1,128)} %copy-done.35, f32[8,18,18,1]{3,2,1,0:T(8,128)} %copy.35, ...), kind=kLoop, calls=%fused_computation.48 | loop fusion | flops 8126456 | bytes 3445024 | tf_op jit(solution)/shard_map/reduce_sum | solution.py:45
  305.5 4.9 %all-reduce.2 = (f32[8]{0:T(128)S(1)}, f32[8]{0:T(128)S(1)}) all-reduce(f32[8]{0:T(128)S(1)} %copy-done.59, f32[8]{0:T(128)S(1)} %fusion.22), channel_id=1, replica_groups=mesh['span'=2,'height'=4,'depth'=4] {'span'}, use_global_device_ids=true, to_apply=%region_9.10 | all-reduce | flops 16 | bytes 128 | tf_op jit(solution)/shard_map/psum | solution.py:50
  310.4 30.6 %all-reduce = (f32[8]{0:T(128)S(1)}, f32[8]{0:T(128)S(1)}) all-reduce(f32[8]{0:T(128)S(1)} %get-tuple-element.15, f32[8]{0:T(128)S(1)} %get-tuple-element.16), channel_id=1, replica_groups=mesh['span'=2,'height'=4,'depth'=4] {'height','depth'}, use_global_device_ids=true, to_apply=%region_10.11 | all-reduce | flops 16 | bytes 128 | tf_op jit(solution)/shard_map/psum | solution.py:49
  342.0 3.4 collective-permute-start.18
  347.8 3.0 collective-permute-start.29
  350.8 2.9 collective-permute-start.28
  363.5 3.0 copy.38
  366.5 3.0 collective-permute-start.22
  371.1 2.8 collective-permute-start.23
  379.7 3.2 fusion.5
  385.0 41.3 %pmax.7 = f32[]{:T(128)} all-reduce(f32[]{:T(128)} %get-tuple-element.19), channel_id=1, replica_groups=mesh['span'=2,'height'=4,'depth'=4] {'span','height','depth'}, use_global_device_ids=true, to_apply=%region_21.22 | all-reduce | flops 1 | bytes 8 | tf_op jit(solution)/shard_map/pmax | solution.py:144
  430.3 4.2 collective-permute-done.30
  438.9 2.6 collective-permute-done.32
  441.6 3.5 collective-permute-start.35
  448.2 3.5 collective-permute-done.34
  (247 shorter events, 102.0 us)
Async XLA Ops:
  5.8 15.1 %collective-permute-start = (f32[2,1,16,128]{3,2,1,0:T(8,128)S(1)}, f32[2,1,16,128]{3,2,1,0:T(8,128)S(1)}, u32[]{:S(2)}, u32[]{:S(2)}) collective-permute-start(f32[2,1,16,128]{3,2,1,0:T(8,128)S(1)} %get-tuple-element.53), channel_id=1, source_target_pairs={{16,0},{17,1},{18,2},{19,3},{20,4},{21,5},{22,6},{23,7},{24,8},{25... | collective-permute-start | bytes 49160 | tf_op jit(solution)/shard_map/ppermute | solution.py:24
  8.2 12.6 %collective-permute-start.2 = (f32[2,1,16,128]{3,2,1,0:T(8,128)S(1)}, f32[2,1,16,128]{3,2,1,0:T(8,128)S(1)}, u32[]{:S(2)}, u32[]{:S(2)}) collective-permute-start(f32[2,1,16,128]{3,2,1,0:T(8,128)S(1)} %get-tuple-element.52), channel_id=1, source_target_pairs={{0,16},{1,17},{2,18},{3,19},{4,20},{5,21},{6,22},{7,23},{8,24},{9,... | collective-permute-start | bytes 49160 | tf_op jit(solution)/shard_map/ppermute | solution.py:21
  20.8 36.5 %copy-start.21 = (f32[2,1,16,128]{3,2,1,0:T(8,128)}, f32[2,1,16,128]{3,2,1,0:T(8,128)S(1)}, u32[]{:S(2)}) copy-start(f32[2,1,16,128]{3,2,1,0:T(8,128)S(1)} %collective-permute-done.2) | copy-start | bytes 49156
  20.9 17.6 %collective-permute-start.4 = (f32[2,18,1,128]{3,2,1,0:T(1,128)S(1)}, f32[2,18,1,128]{3,2,1,0:T(1,128)S(1)}, u32[]{:S(2)}, u32[]{:S(2)}) collective-permute-start(f32[2,18,1,128]{3,2,1,0:T(1,128)S(1)} %get-tuple-element.51), channel_id=1, source_target_pairs={{4,0},{8,4},{12,8},{5,1},{9,5},{13,9},{6,2},{10,6},{14,10},{7,3},{... | collective-permute-start | bytes 55304 | tf_op jit(solution)/shard_map/ppermute | solution.py:24
  22.8 15.7 %collective-permute-start.6 = (f32[2,18,1,128]{3,2,1,0:T(1,128)S(1)}, f32[2,18,1,128]{3,2,1,0:T(1,128)S(1)}, u32[]{:S(2)}, u32[]{:S(2)}) collective-permute-start(f32[2,18,1,128]{3,2,1,0:T(1,128)S(1)} %get-tuple-element.50), channel_id=1, source_target_pairs={{0,4},{4,8},{8,12},{1,5},{5,9},{9,13},{2,6},{6,10},{10,14},{3,7},{... | collective-permute-start | bytes 55304 | tf_op jit(solution)/shard_map/ppermute | solution.py:21
  32.5 13.9 %all-to-all-start = ((bf16[16,8,512]{2,1,0:T(8,128)(2,1)}), bf16[16,8,512]{2,1,0:T(8,128)(2,1)S(1)}, u32[]{:S(2)}, u32[]{:S(2)}) async-start(bf16[16,8,512]{2,1,0:T(8,128)(2,1)} %copy.23), calls=%async_computation | async-start | bytes 262144 | tf_op jit(solution)/shard_map/all_to_all | solution.py:106
  38.5 18.8 %copy-start.30 = (f32[2,18,1,128]{3,2,1,0:T(1,128)}, f32[2,18,1,128]{3,2,1,0:T(1,128)S(1)}, u32[]{:S(2)}) copy-start(f32[2,18,1,128]{3,2,1,0:T(1,128)S(1)} %collective-permute-done.6) | copy-start | bytes 55300
  39.6 69.7 %collective-permute-start.10 = (f32[2,18,18,1]{3,2,1,0:T(8,128)}, f32[2,18,18,1]{3,2,1,0:T(8,128)}, u32[]{:S(2)}, u32[]{:S(2)}) collective-permute-start(f32[2,18,18,1]{3,2,1,0:T(8,128)} %get-tuple-element.49), channel_id=1, source_target_pairs={{0,1},{1,2},{2,3},{4,5},{5,6},{6,7},{8,9},{9,10},{10,11},{12,13},{... | collective-permute-start | bytes 7784 | tf_op jit(solution)/shard_map/ppermute | solution.py:21
  43.1 83.0 %collective-permute-start.8 = (f32[2,18,18,1]{3,2,1,0:T(8,128)}, f32[2,18,18,1]{3,2,1,0:T(8,128)}, u32[]{:S(2)}, u32[]{:S(2)}) collective-permute-start(f32[2,18,18,1]{3,2,1,0:T(8,128)} %get-tuple-element.48), channel_id=1, source_target_pairs={{1,0},{2,1},{3,2},{5,4},{6,5},{7,6},{9,8},{10,9},{11,10},{13,12},{... | collective-permute-start | bytes 7784 | tf_op jit(solution)/shard_map/ppermute | solution.py:24
  52.7 7.9 %all-to-all-start.1 = ((f32[16,8,512]{2,1,0:T(8,128)}), f32[16,8,512]{2,1,0:T(8,128)}, u32[]{:S(2)}, u32[]{:S(2)}) async-start(f32[16,8,512]{2,1,0:T(8,128)} %fusion.123), calls=%async_computation.1 | async-start | bytes 524288 | tf_op jit(solution)/shard_map/all_to_all | solution.py:95
  95.8 6.7 %collective-permute-start.3 = (f32[8,1,16,128]{3,2,1,0:T(8,128)S(1)}, f32[8,1,16,128]{3,2,1,0:T(8,128)S(1)}, u32[]{:S(2)}, u32[]{:S(2)}) collective-permute-start(f32[8,1,16,128]{3,2,1,0:T(8,128)S(1)} %get-tuple-element.43), channel_id=1, source_target_pairs={{0,16},{1,17},{2,18},{3,19},{4,20},{5,21},{6,22},{7,23},{8,24},{9,... | collective-permute-start | bytes 196616 | tf_op jit(solution)/shard_map/ppermute | solution.py:21
  98.0 6.4 %collective-permute-start.1 = (f32[8,1,16,128]{3,2,1,0:T(8,128)S(1)}, f32[8,1,16,128]{3,2,1,0:T(8,128)S(1)}, u32[]{:S(2)}, u32[]{:S(2)}) collective-permute-start(f32[8,1,16,128]{3,2,1,0:T(8,128)S(1)} %get-tuple-element.42), channel_id=1, source_target_pairs={{16,0},{17,1},{18,2},{19,3},{20,4},{21,5},{22,6},{23,7},{24,8},{25... | collective-permute-start | bytes 196616 | tf_op jit(solution)/shard_map/ppermute | solution.py:24
  105.0 6.2 %collective-permute-start.5 = (f32[8,18,1,128]{3,2,1,0:T(1,128)S(1)}, f32[8,18,1,128]{3,2,1,0:T(1,128)S(1)}, u32[]{:S(2)}, u32[]{:S(2)}) collective-permute-start(f32[8,18,1,128]{3,2,1,0:T(1,128)S(1)} %get-tuple-element.35), channel_id=1, source_target_pairs={{4,0},{8,4},{12,8},{5,1},{9,5},{13,9},{6,2},{10,6},{14,10},{7,3},{... | collective-permute-start | bytes 221192 | tf_op jit(solution)/shard_map/ppermute | solution.py:24
  107.2 5.7 %collective-permute-start.7 = (f32[8,18,1,128]{3,2,1,0:T(1,128)S(1)}, f32[8,18,1,128]{3,2,1,0:T(1,128)S(1)}, u32[]{:S(2)}, u32[]{:S(2)}) collective-permute-start(f32[8,18,1,128]{3,2,1,0:T(1,128)S(1)} %get-tuple-element.34), channel_id=1, source_target_pairs={{0,4},{4,8},{8,12},{1,5},{5,9},{9,13},{2,6},{6,10},{10,14},{3,7},{... | collective-permute-start | bytes 221192 | tf_op jit(solution)/shard_map/ppermute | solution.py:21
  117.9 10.2 %collective-permute-start.11 = (f32[8,18,18,1]{2,0,3,1:T(8,128)S(1)}, f32[8,18,18,1]{2,0,3,1:T(8,128)S(1)}, u32[]{:S(2)}, u32[]{:S(2)}) collective-permute-start(f32[8,18,18,1]{2,0,3,1:T(8,128)S(1)} %copy.28), channel_id=1, source_target_pairs={{0,1},{1,2},{2,3},{4,5},{5,6},{6,7},{8,9},{9,10},{10,11},{12,13},{... | collective-permute-start | bytes 31112 | tf_op jit(solution)/shard_map/ppermute | solution.py:21
  123.0 7.3 %collective-permute-start.9 = (f32[8,18,18,1]{2,0,3,1:T(8,128)S(1)}, f32[8,18,18,1]{2,0,3,1:T(8,128)S(1)}, u32[]{:S(2)}, u32[]{:S(2)}) collective-permute-start(f32[8,18,18,1]{2,0,3,1:T(8,128)S(1)} %copy.26), channel_id=1, source_target_pairs={{1,0},{2,1},{3,2},{5,4},{6,5},{7,6},{9,8},{10,9},{11,10},{13,12},{... | collective-permute-start | bytes 31112 | tf_op jit(solution)/shard_map/ppermute | solution.py:24
  138.5 50.8 %copy-start.3 = (f32[8,16,16,128]{3,2,1,0:T(8,128)}, f32[8,16,16,128]{3,2,1,0:T(8,128)S(1)}, u32[]{:S(2)}) copy-start(f32[8,16,16,128]{3,2,1,0:T(8,128)S(1)} %get-tuple-element.23) | copy-start | bytes 3145732
  240.4 24.9 %copy-start.2 = (f32[8,16,16,128]{3,2,1,0:T(8,128)S(1)}, f32[8,16,16,128]{3,2,1,0:T(8,128)}, u32[]{:S(2)}) copy-start(f32[8,16,16,128]{3,2,1,0:T(8,128)} %param.5) | copy-start | bytes 3145732
  252.3 12.4 %collective-permute-start.13 = (f32[8,1,16,128]{3,2,1,0:T(8,128)S(1)}, f32[8,1,16,128]{3,2,1,0:T(8,128)S(1)}, u32[]{:S(2)}, u32[]{:S(2)}) collective-permute-start(f32[8,1,16,128]{3,2,1,0:T(8,128)S(1)} %get-tuple-element.39), channel_id=1, source_target_pairs={{0,16},{1,17},{2,18},{3,19},{4,20},{5,21},{6,22},{7,23},{8,24},{9,... | collective-permute-start | bytes 196616 | tf_op jit(solution)/shard_map/ppermute | solution.py:21
  254.3 17.7 %collective-permute-start.25 = (bf16[1,16,128]{2,1,0:T(8,128)(2,1)S(1)}, bf16[1,16,128]{2,1,0:T(8,128)(2,1)S(1)}, u32[]{:S(2)}, u32[]{:S(2)}) collective-permute-start(bf16[1,16,128]{2,1,0:T(8,128)(2,1)S(1)} %get-tuple-element.67), channel_id=1, source_target_pairs={{16,0},{17,1},{18,2},{19,3},{20,4},{21,5},{22,6},{23,7},{24,8},{25... | collective-permute-start | bytes 12296 | tf_op jit(solution)/shard_map/ppermute | solution.py:24
  258.9 13.2 %collective-permute-start.24 = (bf16[1,16,128]{2,1,0:T(8,128)(2,1)S(1)}, bf16[1,16,128]{2,1,0:T(8,128)(2,1)S(1)}, u32[]{:S(2)}, u32[]{:S(2)}) collective-permute-start(bf16[1,16,128]{2,1,0:T(8,128)(2,1)S(1)} %get-tuple-element.66), channel_id=1, source_target_pairs={{0,16},{1,17},{2,18},{3,19},{4,20},{5,21},{6,22},{7,23},{8,24},{9,... | collective-permute-start | bytes 12296 | tf_op jit(solution)/shard_map/ppermute | solution.py:21
  260.2 7.4 %collective-permute-start.12 = (f32[8,1,16,128]{3,2,1,0:T(8,128)S(1)}, f32[8,1,16,128]{3,2,1,0:T(8,128)S(1)}, u32[]{:S(2)}, u32[]{:S(2)}) collective-permute-start(f32[8,1,16,128]{3,2,1,0:T(8,128)S(1)} %get-tuple-element.38), channel_id=1, source_target_pairs={{16,0},{17,1},{18,2},{19,3},{20,4},{21,5},{22,6},{23,7},{24,8},{25... | collective-permute-start | bytes 196616 | tf_op jit(solution)/shard_map/ppermute | solution.py:24
  267.7 9.7 %collective-permute-start.14 = (f32[8,18,1,128]{3,2,1,0:T(1,128)S(1)}, f32[8,18,1,128]{3,2,1,0:T(1,128)S(1)}, u32[]{:S(2)}, u32[]{:S(2)}) collective-permute-start(f32[8,18,1,128]{3,2,1,0:T(1,128)S(1)} %get-tuple-element.33), channel_id=1, source_target_pairs={{4,0},{8,4},{12,8},{5,1},{9,5},{13,9},{6,2},{10,6},{14,10},{7,3},{... | collective-permute-start | bytes 221192 | tf_op jit(solution)/shard_map/ppermute | solution.py:24
  269.6 7.8 %collective-permute-start.15 = (f32[8,18,1,128]{3,2,1,0:T(1,128)S(1)}, f32[8,18,1,128]{3,2,1,0:T(1,128)S(1)}, u32[]{:S(2)}, u32[]{:S(2)}) collective-permute-start(f32[8,18,1,128]{3,2,1,0:T(1,128)S(1)} %get-tuple-element.32), channel_id=1, source_target_pairs={{0,4},{4,8},{8,12},{1,5},{5,9},{9,13},{2,6},{6,10},{10,14},{3,7},{... | collective-permute-start | bytes 221192 | tf_op jit(solution)/shard_map/ppermute | solution.py:21
  272.1 21.2 %collective-permute-start.27 = (bf16[18,1,128]{2,1,0:T(2,128)(2,1)S(1)}, bf16[18,1,128]{2,1,0:T(2,128)(2,1)S(1)}, u32[]{:S(2)}, u32[]{:S(2)}) collective-permute-start(bf16[18,1,128]{2,1,0:T(2,128)(2,1)S(1)} %get-tuple-element.63), channel_id=1, source_target_pairs={{4,0},{8,4},{12,8},{5,1},{9,5},{13,9},{6,2},{10,6},{14,10},{7,3},{... | collective-permute-start | bytes 13832 | tf_op jit(solution)/shard_map/ppermute | solution.py:24
  275.3 18.0 %collective-permute-start.26 = (bf16[18,1,128]{2,1,0:T(2,128)(2,1)S(1)}, bf16[18,1,128]{2,1,0:T(2,128)(2,1)S(1)}, u32[]{:S(2)}, u32[]{:S(2)}) collective-permute-start(bf16[18,1,128]{2,1,0:T(2,128)(2,1)S(1)} %get-tuple-element.62), channel_id=1, source_target_pairs={{0,4},{4,8},{8,12},{1,5},{5,9},{9,13},{2,6},{6,10},{10,14},{3,7},{... | collective-permute-start | bytes 13832 | tf_op jit(solution)/shard_map/ppermute | solution.py:21
  283.8 10.3 %collective-permute-start.17 = (f32[8,18,18,1]{2,0,3,1:T(8,128)}, f32[8,18,18,1]{2,0,3,1:T(8,128)}, u32[]{:S(2)}, u32[]{:S(2)}) collective-permute-start(f32[8,18,18,1]{2,0,3,1:T(8,128)} %copy.36), channel_id=1, source_target_pairs={{0,1},{1,2},{2,3},{4,5},{5,6},{6,7},{8,9},{9,10},{10,11},{12,13},{... | collective-permute-start | bytes 31112 | tf_op jit(solution)/shard_map/ppermute | solution.py:21
  288.8 8.5 %collective-permute-start.16 = (f32[8,18,18,1]{2,0,3,1:T(8,128)}, f32[8,18,18,1]{2,0,3,1:T(8,128)}, u32[]{:S(2)}, u32[]{:S(2)}) collective-permute-start(f32[8,18,18,1]{2,0,3,1:T(8,128)} %copy.34), channel_id=1, source_target_pairs={{1,0},{2,1},{3,2},{5,4},{6,5},{7,6},{9,8},{10,9},{11,10},{13,12},{... | collective-permute-start | bytes 31112 | tf_op jit(solution)/shard_map/ppermute | solution.py:24
  300.4 40.6 %copy-start.60 = (f32[8]{0:T(128)S(1)}, f32[8]{0:T(128)}, u32[]{:S(2)}) copy-start(f32[8]{0:T(128)} %get-tuple-element.13) | copy-start | bytes 100
  300.4 40.6 %copy-start.61 = (f32[8]{0:T(128)S(1)}, f32[8]{0:T(128)}, u32[]{:S(2)}) copy-start(f32[8]{0:T(128)} %get-tuple-element.14) | copy-start | bytes 100
  341.9 37.8 %copy-start = (f32[8,16,16,128]{3,2,1,0:T(8,128)}, f32[8,16,16,128]{3,2,1,0:T(8,128)S(1)}, u32[]{:S(2)}) copy-start(f32[8,16,16,128]{3,2,1,0:T(8,128)S(1)} %multiply_add_fusion) | copy-start | bytes 3145732
  341.9 16.2 %copy-start.20 = (bf16[16,16,128]{2,1,0:T(8,128)(2,1)S(1)}, bf16[16,16,128]{2,1,0:T(8,128)(2,1)}, u32[]{:S(2)}) copy-start(bf16[16,16,128]{2,1,0:T(8,128)(2,1)} %get-tuple-element.54) | copy-start | bytes 196612
  342.0 11.7 %collective-permute-start.18 = (f32[8,1,16,128]{3,2,1,0:T(8,128)S(1)}, f32[8,1,16,128]{3,2,1,0:T(8,128)S(1)}, u32[]{:S(2)}, u32[]{:S(2)}) collective-permute-start(f32[8,1,16,128]{3,2,1,0:T(8,128)S(1)} %get-tuple-element.37), channel_id=1, source_target_pairs={{16,0},{17,1},{18,2},{19,3},{20,4},{21,5},{22,6},{23,7},{24,8},{25... | collective-permute-start | bytes 196616 | tf_op jit(solution)/shard_map/ppermute | solution.py:24
  345.4 8.2 %collective-permute-start.19 = (f32[8,1,16,128]{3,2,1,0:T(8,128)S(1)}, f32[8,1,16,128]{3,2,1,0:T(8,128)S(1)}, u32[]{:S(2)}, u32[]{:S(2)}) collective-permute-start(f32[8,1,16,128]{3,2,1,0:T(8,128)S(1)} %get-tuple-element.36), channel_id=1, source_target_pairs={{0,16},{1,17},{2,18},{3,19},{4,20},{5,21},{6,22},{7,23},{8,24},{9,... | collective-permute-start | bytes 196616 | tf_op jit(solution)/shard_map/ppermute | solution.py:21
  347.8 10.3 %collective-permute-start.29 = (bf16[18,18,1]{2,1,0:T(8,128)(2,1)S(1)}, bf16[18,18,1]{2,1,0:T(8,128)(2,1)S(1)}, u32[]{:S(2)}, u32[]{:S(2)}) collective-permute-start(bf16[18,18,1]{2,1,0:T(8,128)(2,1)S(1)} %get-tuple-element.59), channel_id=1, source_target_pairs={{1,0},{2,1},{3,2},{5,4},{6,5},{7,6},{9,8},{10,9},{11,10},{13,12},{... | collective-permute-start | bytes 1952 | tf_op jit(solution)/shard_map/ppermute | solution.py:24
  350.8 7.4 %collective-permute-start.28 = (bf16[18,18,1]{2,1,0:T(8,128)(2,1)S(1)}, bf16[18,18,1]{2,1,0:T(8,128)(2,1)S(1)}, u32[]{:S(2)}, u32[]{:S(2)}) collective-permute-start(bf16[18,18,1]{2,1,0:T(8,128)(2,1)S(1)} %get-tuple-element.58), channel_id=1, source_target_pairs={{0,1},{1,2},{2,3},{4,5},{5,6},{6,7},{8,9},{9,10},{10,11},{12,13},{... | collective-permute-start | bytes 1952 | tf_op jit(solution)/shard_map/ppermute | solution.py:21
  353.8 5.4 %collective-permute-start.20 = (f32[8,18,1,128]{3,2,1,0:T(1,128)S(1)}, f32[8,18,1,128]{3,2,1,0:T(1,128)S(1)}, u32[]{:S(2)}, u32[]{:S(2)}) collective-permute-start(f32[8,18,1,128]{3,2,1,0:T(1,128)S(1)} %get-tuple-element.31), channel_id=1, source_target_pairs={{4,0},{8,4},{12,8},{5,1},{9,5},{13,9},{6,2},{10,6},{14,10},{7,3},{... | collective-permute-start | bytes 221192 | tf_op jit(solution)/shard_map/ppermute | solution.py:24
  355.7 5.7 %collective-permute-start.21 = (f32[8,18,1,128]{3,2,1,0:T(1,128)S(1)}, f32[8,18,1,128]{3,2,1,0:T(1,128)S(1)}, u32[]{:S(2)}, u32[]{:S(2)}) collective-permute-start(f32[8,18,1,128]{3,2,1,0:T(1,128)S(1)} %get-tuple-element.30), channel_id=1, source_target_pairs={{0,4},{4,8},{8,12},{1,5},{5,9},{9,13},{2,6},{6,10},{10,14},{3,7},{... | collective-permute-start | bytes 221192 | tf_op jit(solution)/shard_map/ppermute | solution.py:21
  366.5 8.4 %collective-permute-start.22 = (f32[8,18,18,1]{2,0,3,1:T(8,128)}, f32[8,18,18,1]{2,0,3,1:T(8,128)}, u32[]{:S(2)}, u32[]{:S(2)}) collective-permute-start(f32[8,18,18,1]{2,0,3,1:T(8,128)} %copy.38), channel_id=1, source_target_pairs={{1,0},{2,1},{3,2},{5,4},{6,5},{7,6},{9,8},{10,9},{11,10},{13,12},{... | collective-permute-start | bytes 31112 | tf_op jit(solution)/shard_map/ppermute | solution.py:24
  371.1 6.4 %collective-permute-start.23 = (f32[8,18,18,1]{2,0,3,1:T(8,128)}, f32[8,18,18,1]{2,0,3,1:T(8,128)S(1)}, u32[]{:S(2)}, u32[]{:S(2)}) collective-permute-start(f32[8,18,18,1]{2,0,3,1:T(8,128)} %copy.40), channel_id=1, source_target_pairs={{0,1},{1,2},{2,3},{4,5},{5,6},{6,7},{8,9},{9,10},{10,11},{12,13},{... | collective-permute-start | bytes 31112 | tf_op jit(solution)/shard_map/ppermute | solution.py:21
  383.0 44.0 %copy-start.9 = (f32[18,18,130]{2,1,0:T(8,128)S(1)}, f32[18,18,130]{2,1,0:T(8,128)}, u32[]{:S(2)}) copy-start(f32[18,18,130]{2,1,0:T(8,128)} %maximum_convert_fusion) | copy-start | bytes 505444
  385.0 67.9 %copy-start.17 = (f32[16,16,128]{2,1,0:T(8,128)}, f32[16,16,128]{2,1,0:T(8,128)S(1)}, u32[]{:S(2)}) copy-start(f32[16,16,128]{2,1,0:T(8,128)S(1)} %get-tuple-element.20) | copy-start | bytes 393220
  427.3 3.1 collective-permute-start.31
  429.0 5.5 %collective-permute-start.30 = (bf16[1,16,128]{2,1,0:T(8,128)(2,1)S(1)}, bf16[1,16,128]{2,1,0:T(8,128)(2,1)S(1)}, u32[]{:S(2)}, u32[]{:S(2)}) collective-permute-start(bf16[1,16,128]{2,1,0:T(8,128)(2,1)S(1)} %get-tuple-element.64), channel_id=1, source_target_pairs={{0,16},{1,17},{2,18},{3,19},{4,20},{5,21},{6,22},{7,23},{8,24},{9,... | collective-permute-start | bytes 12296 | tf_op jit(solution)/shard_map/ppermute | solution.py:21
  434.5 4.3 collective-permute-start.33
  436.4 5.0 %collective-permute-start.32 = (bf16[18,1,128]{2,1,0:T(2,128)(2,1)S(1)}, bf16[18,1,128]{2,1,0:T(2,128)(2,1)S(1)}, u32[]{:S(2)}, u32[]{:S(2)}) collective-permute-start(bf16[18,1,128]{2,1,0:T(2,128)(2,1)S(1)} %get-tuple-element.60), channel_id=1, source_target_pairs={{0,4},{4,8},{8,12},{1,5},{5,9},{9,13},{2,6},{6,10},{10,14},{3,7},{... | collective-permute-start | bytes 13832 | tf_op jit(solution)/shard_map/ppermute | solution.py:21
  441.6 6.6 %collective-permute-start.35 = (bf16[18,18,1]{2,1,0:T(8,128)(2,1)S(1)}, bf16[18,18,1]{2,1,0:T(8,128)(2,1)S(1)}, u32[]{:S(2)}, u32[]{:S(2)}) collective-permute-start(bf16[18,18,1]{2,1,0:T(8,128)(2,1)S(1)} %get-tuple-element.57), channel_id=1, source_target_pairs={{1,0},{2,1},{3,2},{5,4},{6,5},{7,6},{9,8},{10,9},{11,10},{13,12},{... | collective-permute-start | bytes 1952 | tf_op jit(solution)/shard_map/ppermute | solution.py:24
  445.1 6.6 %collective-permute-start.34 = (bf16[18,18,1]{2,1,0:T(8,128)(2,1)S(1)}, bf16[18,18,1]{2,1,0:T(8,128)(2,1)S(1)}, u32[]{:S(2)}, u32[]{:S(2)}) collective-permute-start(bf16[18,18,1]{2,1,0:T(8,128)(2,1)S(1)} %get-tuple-element.56), channel_id=1, source_target_pairs={{0,1},{1,2},{2,3},{4,5},{5,6},{6,7},{8,9},{9,10},{10,11},{12,13},{... | collective-permute-start | bytes 1952 | tf_op jit(solution)/shard_map/ppermute | solution.py:21
  (52 other events, 404.4 us)
